TPU v7x, 16 devices: a whole 2x2x2 slice. The times are simulated.
16 devices in a mesh: dp: 2 (over z), tp: 8 (over y, x, core).
Axes of the slice: x: 2, y: 2, z: 2, core: 2. Of those that a mesh axis runs over, the one named last changes fastest.
Arguments:
- hidden: bfloat16 [6, 128, 6144], P('dp', 'tp'), parts along dimension 0
- ln1_gain: float32 [6144], replicated
- ln1_bias: float32 [6144], replicated
- w_qkv: bfloat16 [6144, 3, 48, 128], P(None, None, 'tp')
- b_qkv: bfloat16 [3, 48, 128], P(None, 'tp')
- w_out: bfloat16 [48, 128, 6144], P('tp')
- b_out: bfloat16 [6144], replicated
- ln2_gain: float32 [6144], replicated
- ln2_bias: float32 [6144], replicated
- w_up: bfloat16 [6144, 24576], P(None, 'tp')
- b_up: bfloat16 [24576], P('tp')
- w_down: bfloat16 [24576, 6144], P('tp')
- b_down: bfloat16 [6144], replicated
Outputs:
- output: bfloat16 [6, 128, 6144], P('dp', 'tp'), parts along dimension 0
There are 2 independent parts. A program takes and returns all parts, laid end to end along the dimension named above; an argument that names none is the same for every part.
All inputs are finite; a program needn't handle non-finite values.
Results may differ from a plain program's by a relative error of at most 0.0102007.
Values are sent between devices in bfloat16 or wider.
A program may use at most 1 GiB of HBM per device.

v0:
```python
import jax
import jax.numpy as jnp
from jax import lax
from jax.sharding import PartitionSpec as P

LN_EPS = 1e-5


def layer_norm(inputs, gain_vec, shift_vec):
    as_f32 = inputs.astype(jnp.float32)
    row_mean = jnp.mean(as_f32, axis=-1, keepdims=True)
    centered = as_f32 - row_mean
    variance = jnp.mean(centered * centered, axis=-1, keepdims=True)
    return (centered * lax.rsqrt(variance + LN_EPS) * gain_vec + shift_vec).astype(jnp.bfloat16)


def causal_attention(queries, keys_all, values):
    seq_len = queries.shape[1]
    head_dim = queries.shape[3]
    logits = jnp.einsum("bqhd,bkhd->bhqk", queries, keys_all, preferred_element_type=jnp.float32) * head_dim ** -0.5
    causal = lax.broadcasted_iota(jnp.int32, (seq_len, seq_len), 0) >= lax.broadcasted_iota(jnp.int32, (seq_len, seq_len), 1)
    logits = jnp.where(causal, logits, -1e30)
    row_max = jnp.max(logits, axis=-1, keepdims=True)
    exp_vals = jnp.exp(logits - row_max)
    weights_bf = (exp_vals / jnp.sum(exp_vals, axis=-1, keepdims=True)).astype(jnp.bfloat16)
    return jnp.einsum("bhqk,bkhd->bqhd", weights_bf, values, preferred_element_type=jnp.float32).astype(jnp.bfloat16)


def solution(mesh):
    group_size = mesh.shape["tp"]

    def scatter_sum(partial):
        n_batch, seq_len, feat_dim = partial.shape
        split_view = partial.astype(jnp.bfloat16).reshape(n_batch, group_size, seq_len // group_size, feat_dim)
        received = lax.all_to_all(split_view, "tp", 1, 1, tiled=True)
        return jnp.sum(received.astype(jnp.float32), axis=1)

    def device_body(hidden, ln1_gain, ln1_bias, w_qkv, b_qkv, w_out, b_out, ln2_gain, ln2_bias, w_up, b_up, w_down, b_down):
        normed = layer_norm(hidden, ln1_gain, ln1_bias)
        normed_all = lax.all_gather(normed, "tp", axis=1, tiled=True)
        qkv_acc = jnp.einsum("bsd,dthe->bsthe", normed_all, w_qkv, preferred_element_type=jnp.float32)
        qkv_all = (qkv_acc + b_qkv.astype(jnp.float32)).astype(jnp.bfloat16)
        context = causal_attention(qkv_all[:, :, 0], qkv_all[:, :, 1], qkv_all[:, :, 2])
        attn_part = jnp.einsum("bqhd,hde->bqe", context, w_out, preferred_element_type=jnp.float32)
        attn_sum = scatter_sum(attn_part)
        resid_mid = (hidden.astype(jnp.float32) + (attn_sum + b_out.astype(jnp.float32))).astype(jnp.bfloat16)
        normed_mid = layer_norm(resid_mid, ln2_gain, ln2_bias)
        mid_all = lax.all_gather(normed_mid, "tp", axis=1, tiled=True)
        up_proj = jnp.einsum("bsd,df->bsf", mid_all, w_up, preferred_element_type=jnp.float32) + b_up.astype(jnp.float32)
        gelu_out = jax.nn.gelu(up_proj, approximate=True).astype(jnp.bfloat16)
        down_part = jnp.einsum("bsf,fd->bsd", gelu_out, w_down, preferred_element_type=jnp.float32)
        down_sum = scatter_sum(down_part)
        return (resid_mid.astype(jnp.float32) + (down_sum + b_down.astype(jnp.float32))).astype(jnp.bfloat16)

    in_layout = (P("dp", "tp", None), P(), P(), P(None, None, "tp", None), P(None, "tp", None), P("tp", None, None), P(), P(), P(), P(None, "tp"), P("tp"), P("tp", None), P())
    layer_fn = jax.shard_map(device_body, mesh=mesh, in_specs=in_layout, out_specs=P("dp", "tp", None), check_vma=False)
    return layer_fn
```

profile of v0, /device:TPU:0, one launch (start us, length us, event | category | flops | bytes accessed | tf_op | source)
XLA Modules:
  0.0 293.2 jit_solution(11910069234107567922)
XLA Ops:
  6.5 1.2 convert_reduce_fusion.3
  7.8 1.4 fusion.41
  9.2 2.2 fusion.44
  11.4 37.7 %all-gather.3.cloned.1.call-done = bf16[3,128,6144]{2,1,0:T(8,128)(2,1)} async-done(((bf16[3,16,6144]{2,1,0:T(8,128)(2,1)}), bf16[3,128,6144]{2,1,0:T(8,128)(2,1)}) %all-gather.3.cloned.1.call-update) | async-done | bytes 4718608 | tf_op jit(solution)/shard_map/all_gather | solution.py:40
  49.1 16.5 %add_convert_fusion = bf16[3,128,3,6,128]{4,1,3,2,0:T(8,128)(2,1)S(1)} fusion(bf16[6144,3,6,128]{3,0,2,1:T(8,128)(2,1)} %param.16, bf16[3,128,6144]{2,1,0:T(8,128)(2,1)} %all-gather.3.cloned.1.call-done, f32[3,6,128]{2,1,0:T(8,128)S(1)} %convert_element_type.61), kind=kOutput, calls=%fused_computation.23 | convolution fusion | flops 10873405440 | bytes 34808832 | tf_op jit(solution)/shard_map/bsd,dthe->bsthe/dot_general | solution.py:41
  65.6 0.5 fusion.35
  66.2 0.2 fusion.52
  66.4 8.5 %bitcast_convert_fusion = bf16[3,128,6144]{2,1,0:T(8,128)(2,1)} fusion(bf16[6,128,6144]{2,1,0:T(8,128)(2,1)} %param.18, bf16[3,128,3,6,128]{4,1,3,2,0:T(8,128)(2,1)S(1)} %add_convert_fusion, f32[3,6,128]{2,1,0:T(8,128)S(1)} %fusion.52, f32[3,6,128,128]{2,3,1,0:T(8,128)S(1)} %fusion.35), kind=kOutput, calls=%fused_computation.7 | convolution fusion | flops 3702917632 | bytes 17114112 | tf_op jit(solution)/shard_map/bqhd,hde->bqe/dot_general | solution.py:44
  74.9 5.0 %copy.14 = bf16[3,8,16,6144]{3,2,0,1:T(8,128)(2,1)} copy(bf16[3,8,16,6144]{3,2,1,0:T(8,128)(2,1)} %bitcast.50) | data formatting | bytes 9437184 | tf_op jit(solution)/shard_map/reshape | solution.py:34
  79.9 4.7 %all-to-all-start = ((bf16[3,8,16,6144]{3,2,0,1:T(8,128)(2,1)}), bf16[3,8,16,6144]{3,2,0,1:T(8,128)(2,1)}, u32[]{:S(2)}, u32[]{:S(2)}) async-start(bf16[3,8,16,6144]{3,2,0,1:T(8,128)(2,1)} %copy.14), calls=%async_computation | async-start | bytes 9437184 | tf_op jit(solution)/shard_map/all_to_all | solution.py:35
  84.7 0.2 all-gather.5.cloned.1.call-start
  84.9 54.4 %all-to-all-done = bf16[3,8,16,6144]{3,2,0,1:T(8,128)(2,1)} async-done(((bf16[3,8,16,6144]{3,2,0,1:T(8,128)(2,1)}), bf16[3,8,16,6144]{3,2,0,1:T(8,128)(2,1)}, u32[]{:S(2)}, u32[]{:S(2)}) %all-to-all-start) | async-done | bytes 4718624 | tf_op jit(solution)/shard_map/all_to_all | solution.py:35
  139.3 3.2 %convert_reduce_fusion.1 = f32[3,16,6144]{2,1,0:T(8,128)S(1)} fusion(bf16[3,8,16,6144]{3,2,0,1:T(8,128)(2,1)} %all-to-all-done), kind=kLoop, calls=%fused_computation.11 | loop fusion | flops 4423680 | bytes 5898240 | tf_op jit(solution)/shard_map/reduce_sum | solution.py:36
  142.5 0.3 convert_reduce_fusion.2
  142.9 0.3 fusion.37
  143.3 1.1 fusion.40
  144.4 34.0 %all-gather.5.cloned.1.call-done = bf16[3,128,6144]{2,1,0:T(8,128)(2,1)} async-done(((bf16[3,16,6144]{2,1,0:T(8,128)(2,1)}), bf16[3,128,6144]{2,1,0:T(8,128)(2,1)}) %all-gather.5.cloned.1.call-update) | async-done | bytes 4718608 | tf_op jit(solution)/shard_map/all_gather | solution.py:48
  178.4 22.1 %fusion.21 = bf16[3,128,3072]{2,1,0:T(8,128)(2,1)S(1)} fusion(bf16[3,128,6144]{2,1,0:T(8,128)(2,1)} %all-gather.5.cloned.1.call-done, bf16[6144,3072]{1,0:T(8,128)(2,1)} %param.22, f32[3072]{0:T(1024)S(1)} %convert_element_type.72), kind=kOutput, calls=%fused_computation.21 | convolution fusion | flops 14507311104 | bytes 44838912 | tf_op jit(solution)/shard_map/bsd,df->bsf/dot_general | solution.py:49
  200.5 19.8 %fusion.11 = bf16[3,128,6144]{2,1,0:T(8,128)(2,1)S(1)} fusion(bf16[3,128,3072]{2,1,0:T(8,128)(2,1)S(1)} %fusion.21, bf16[3072,6144]{1,0:T(8,128)(2,1)} %param.24), kind=kOutput, calls=%fused_computation.12 | convolution fusion | flops 14497873920 | bytes 44826624 | tf_op jit(solution)/shard_map/bsf,fd->bsd/dot_general | solution.py:51
  220.3 2.5 copy.15
  222.8 4.7 %all-to-all-start.1 = ((bf16[3,8,16,6144]{3,2,0,1:T(8,128)(2,1)}), bf16[3,8,16,6144]{3,2,0,1:T(8,128)(2,1)}, u32[]{:S(2)}, u32[]{:S(2)}) async-start(bf16[3,8,16,6144]{3,2,0,1:T(8,128)(2,1)} %copy.15), calls=%async_computation.1 | async-start | bytes 9437184 | tf_op jit(solution)/shard_map/all_to_all | solution.py:35
  227.6 54.6 %all-to-all-done.1 = bf16[3,8,16,6144]{3,2,0,1:T(8,128)(2,1)} async-done(((bf16[3,8,16,6144]{3,2,0,1:T(8,128)(2,1)}), bf16[3,8,16,6144]{3,2,0,1:T(8,128)(2,1)}, u32[]{:S(2)}, u32[]{:S(2)}) %all-to-all-start.1) | async-done | bytes 4718624 | tf_op jit(solution)/shard_map/all_to_all | solution.py:35
  282.2 3.2 %convert_reduce_fusion = f32[3,16,6144]{2,1,0:T(8,128)S(1)} fusion(bf16[3,8,16,6144]{3,2,0,1:T(8,128)(2,1)} %all-to-all-done.1), kind=kLoop, calls=%fused_computation.10 | loop fusion | flops 4423680 | bytes 5898240 | tf_op jit(solution)/shard_map/reduce_sum | solution.py:36
  285.3 1.0 fusion.46
  (26 shorter events, 0.2 us)
Async XLA Ops:
  6.5 4.9 %copy-start.5 = (bf16[3,6,128]{2,1,0:T(8,128)(2,1)S(1)}, bf16[3,6,128]{2,1,0:T(8,128)(2,1)}, u32[]{:S(2)}) copy-start(bf16[3,6,128]{2,1,0:T(8,128)(2,1)} %param.17) | copy-start | bytes 13828
  6.5 42.6 %all-gather.3.cloned.1.call-start = ((), (), s32[]{:S(2)}) async-start(), calls=%async_computation.2 | async-start | bytes 5308416 | tf_op jit(solution)/shard_map/all_gather | solution.py:40
  79.9 5.0 %copy-start.3 = (bf16[6144]{0:T(1024)(128)(2,1)S(1)}, bf16[6144]{0:T(1024)(128)(2,1)}, u32[]{:S(2)}) copy-start(bf16[6144]{0:T(1024)(128)(2,1)} %param.19) | copy-start | bytes 36868
  79.9 59.4 %all-to-all-start = ((bf16[3,8,16,6144]{3,2,0,1:T(8,128)(2,1)}), bf16[3,8,16,6144]{3,2,0,1:T(8,128)(2,1)}, u32[]{:S(2)}, u32[]{:S(2)}) async-start(bf16[3,8,16,6144]{3,2,0,1:T(8,128)(2,1)} %copy.14), calls=%async_computation | async-start | bytes 9437184 | tf_op jit(solution)/shard_map/all_to_all | solution.py:35
  84.7 93.7 %all-gather.5.cloned.1.call-start = ((), (), s32[]{:S(2)}) async-start(), calls=%async_computation.3 | async-start | bytes 5308416 | tf_op jit(solution)/shard_map/all_gather | solution.py:48
  84.9 57.6 %copy-start = (bf16[3,16,6144]{2,1,0:T(8,128)(2,1)S(1)}, bf16[3,16,6144]{2,1,0:T(8,128)(2,1)}, u32[]{:S(2)}) copy-start(bf16[3,16,6144]{2,1,0:T(8,128)(2,1)} %param.13) | copy-start | bytes 1769476
  142.5 0.7 copy-start.1
  142.5 0.7 copy-start.2
  142.9 1.5 copy-start.6
  222.8 4.7 %copy-start.4 = (bf16[6144]{0:T(1024)(128)(2,1)S(1)}, bf16[6144]{0:T(1024)(128)(2,1)}, u32[]{:S(2)}) copy-start(bf16[6144]{0:T(1024)(128)(2,1)} %param.25) | copy-start | bytes 36868
  222.8 59.3 %all-to-all-start.1 = ((bf16[3,8,16,6144]{3,2,0,1:T(8,128)(2,1)}), bf16[3,8,16,6144]{3,2,0,1:T(8,128)(2,1)}, u32[]{:S(2)}, u32[]{:S(2)}) async-start(bf16[3,8,16,6144]{3,2,0,1:T(8,128)(2,1)} %copy.15), calls=%async_computation.1 | async-start | bytes 9437184 | tf_op jit(solution)/shard_map/all_to_all | solution.py:35
Sparse Core Ops, SparseCore 0:
  11.5 37.5 all-gather.2
  144.5 33.8 all-gather.4
where the time goes:
time: 294 us; the launch traced here: 293 us
  waiting for transfers between devices  181 us (62%)
  matrix products  67.5 us (23%)
  other arithmetic  14.2 us (5%)
  between operations  13.6 us (5%)
  starting transfers between devices  9.69 us (3%)
  local copies, waits for them, and re-layouts  7.54 us (3%)
    all_to_all x2, waiting for transfers between devices, scatter_sum(): received = lax.all_to_all(split_view, 'tp', 1, 1, tiled=True)  109 us
    all_gather x1, waiting for transfers between devices, device_body(): normed_all = lax.all_gather(normed, 'tp', axis=1, tiled=True)  37.7 us
    all_gather x1, waiting for transfers between devices, device_body(): mid_all = lax.all_gather(normed_mid, 'tp', axis=1, tiled=True)  34 us
    dot_general x1, matrix products, device_body(): jnp.einsum('bsd,df->bsf', mid_all, w_up, preferred_element_type=jnp.float32)  22.1 us
    dot_general x1, matrix products, device_body(): jnp.einsum('bsf,fd->bsd', gelu_out, w_down, preferred_element_type=jnp.fl...  19.8 us
    dot_general x1, matrix products, device_body(): jnp.einsum('bsd,dthe->bsthe', normed_all, w_qkv, preferred_element_type=j...  16.5 us
    all_to_all x2, starting transfers between devices, scatter_sum(): received = lax.all_to_all(split_view, 'tp', 1, 1, tiled=True)  9.47 us
    dot_general x1, matrix products, device_body(): jnp.einsum('bqhd,hde->bqe', context, w_out, preferred_element_type=jnp.fl...  8.51 us
  transfers between devices with their start and end apart: 4, of which 4 were waited for; matrix products, arithmetic and copies ran while one was open for 0% of the time, Pallas kernels for 0%

commit v1 on v0

v1 whole, which is shorter than its diff:
```python
import functools

import jax
import jax.numpy as jnp
from jax import lax
from jax.experimental import pallas as pl
from jax.experimental.pallas import tpu as pltpu
from jax.sharding import PartitionSpec as P

MESH = pl.DeviceIdType.MESH
F32 = jnp.float32
BF16 = jnp.bfloat16
LN_EPS = 1e-5

N_DEV = 8
B, S_LOC = 3, 16
ROWS = B * S_LOC
M = N_DEV * ROWS
D = 6144
HEADS, HD = 6, 128
NQ = HEADS * HD
FF = 3072
NU = 6
KC = D // NU
NC = 768
NCH = D // NC
NS = 13
T_QKV = NU * 3
T_OUT = T_QKV + NCH
T_UP = T_OUT + NU * (FF // NC)
T_ALL = T_UP + NCH * (FF // KC)


def rows2d(v):
    return v.reshape(-1, v.shape[-1])


def kernel(x_hbm, wq_hbm, wo_hbm, wu_hbm, wd_hbm, g1_ref, c1_ref, bq_ref, bo_ref, g2_ref, c2_ref, bu_ref, bd_ref, out_ref,
           xv, hg1, hg2, acc, qkv, ctx, ub, part, s1, r1a, r1b, s2, r2a, r2b, s3, r3a, r3b, keep, x1, ring,
           x_sem, w_sem, ag_send, ag_recv, rs_send, rs_recv):
    me = lax.axis_index("tp")
    core = lax.rem(me, 2)
    xbit = lax.rem(me // 2, 2)
    ybit = me // 4
    dx = 2 - 4 * xbit
    dy = 4 - 8 * ybit
    ds = 1 - 2 * core
    sis = me + ds
    n1 = me + (1 - core) * dx + core * dy
    n2 = me + (1 - core) * dy + core * dx
    dg = me + dx + dy

    def tile_copies(i, static=None):
        slot = lax.rem(i, NS) if not isinstance(i, int) else i % NS
        buf, sem = ring.at[slot], w_sem.at[slot]

        def q_tile():
            u, t = i // 3, lax.rem(i, 3) if not isinstance(i, int) else i % 3
            k0 = pl.multiple_of(u * KC, KC)
            return [pltpu.make_async_copy(wq_hbm.at[t, h, pl.ds(k0, KC), :], buf.at[:, h * HD:(h + 1) * HD], sem) for h in range(HEADS)]

        def o_tile():
            n0 = pl.multiple_of((i - T_QKV) * NC, NC)
            return [pltpu.make_async_copy(wo_hbm.at[:, pl.ds(n0, NC)], buf.at[0:NQ, :], sem)]

        def u_tile():
            j = i - T_OUT
            k0 = pl.multiple_of((j // 4) * KC, KC)
            n0 = pl.multiple_of(lax.rem(j, 4) * NC if not isinstance(j, int) else (j % 4) * NC, NC)
            return [pltpu.make_async_copy(wu_hbm.at[pl.ds(k0, KC), pl.ds(n0, NC)], buf, sem)]

        def d_tile():
            j = i - T_UP
            n0 = pl.multiple_of((j // 3) * NC, NC)
            k0 = pl.multiple_of(lax.rem(j, 3) * KC if not isinstance(j, int) else (j % 3) * KC, KC)
            return [pltpu.make_async_copy(wd_hbm.at[pl.ds(k0, KC), pl.ds(n0, NC)], buf, sem)]

        return ((0, T_QKV, q_tile), (T_QKV, T_OUT, o_tile), (T_OUT, T_UP, u_tile), (T_UP, T_ALL, d_tile))

    def start_tile(i):
        for lo, hi, make in tile_copies(i):
            if isinstance(i, int):
                if lo <= i < hi:
                    for c in make():
                        c.start()
            else:
                @pl.when(jnp.logical_and(i >= lo, i < hi))
                def _():
                    for c in make():
                        c.start()

    def wait_tile(i, rows=KC):
        slot = lax.rem(i, NS)
        buf = ring.at[slot]
        pltpu.make_async_copy(wu_hbm.at[0:rows, 0:NC], buf.at[0:rows, :], w_sem.at[slot]).wait()
        return buf

    def ag_msg(p, hg, u, j):
        block = (me, me, me, n1, n1, n2, dg)[j]
        to = (n1, n2, sis, n2, sis, sis, sis)[j]
        return pltpu.make_async_remote_copy(
            src_ref=hg.at[u, block], dst_ref=hg.at[u, block], send_sem=ag_send.at[p, u, j], recv_sem=ag_recv.at[p, u, j],
            device_id={"tp": to}, device_id_type=MESH)

    def ag_wait_recv(p, hg, u, j):
        block = (n1, n2, sis, dg, n2 + ds, n1 + ds, dg + ds)[j]
        pltpu.make_async_remote_copy(
            src_ref=hg.at[u, block], dst_ref=hg.at[u, block], send_sem=ag_send.at[p, u, j], recv_sem=ag_recv.at[p, u, j],
            device_id={"tp": me}, device_id_type=MESH).wait_recv()

    def ag_own(p, hg, u):
        for j in (0, 1, 2):
            ag_msg(p, hg, u, j).start()

    def ag_step(p, hg, u, compute):
        @pl.when(u < NU)
        def _():
            ag_wait_recv(p, hg, u, 0)
            ag_msg(p, hg, u, 3).start()
            ag_msg(p, hg, u, 4).start()
            ag_wait_recv(p, hg, u, 1)
            ag_msg(p, hg, u, 5).start()

        @pl.when(u + 2 < NU)
        def _():
            ag_own(p, hg, u + 2)

        @pl.when(jnp.logical_and(u >= 1, u < NU + 1))
        def _():
            ag_wait_recv(p, hg, u - 1, 3)
            ag_msg(p, hg, u - 1, 6).start()

        @pl.when(u >= 2)
        def _():
            for j in (2, 4, 5, 6):
                ag_wait_recv(p, hg, u - 2, j)
            compute(u - 2)

    def ag_drain(p, hg):
        def body(u, _):
            for j in range(7):
                ag_msg(p, hg, u, j).wait_send()
            return 0
        lax.fori_loop(0, NU, body, 0)

    def rs_msg(p, n, j, r1, r2, r3):
        src = (s1, s2, s3)[j]
        dst = (r1, r2, r3)[j]
        to = (sis, n1, n2)[j]
        return pltpu.make_async_remote_copy(
            src_ref=src.at[n], dst_ref=dst.at[n], send_sem=rs_send.at[p, n, j], recv_sem=rs_recv.at[p, n, j],
            device_id={"tp": to}, device_id_type=MESH)

    c_me, c_n1, c_n2, c_dg = me // 2, n1 // 2, n2 // 2, dg // 2

    def rs_phase(p, r1, r2, r3, product, finish):
        def body(n, _):
            @pl.when(n < NCH)
            def _():
                product(n, lax.rem(n, 2))
                for q in range(4):
                    s1[n, q] = part[lax.rem(n, 2), 2 * q + 1 - core].astype(BF16)

                rs_msg(p, n, 0, r1, r2, r3).start()

            @pl.when(jnp.logical_and(n >= 1, n < NCH + 1))
            def _():
                m = n - 1
                rs_msg(p, m, 0, r1, r2, r3).wait_recv()
                slot = lax.rem(m, 2)

                def total(q):
                    return part[slot, 2 * q + core] + r1[m, q].astype(F32)

                s2[m, 0] = total(c_n1).astype(BF16)
                s2[m, 1] = total(c_dg).astype(BF16)
                keep[m, 0] = total(c_me)
                keep[m, 1] = total(c_n2)
                rs_msg(p, m, 1, r1, r2, r3).start()

            @pl.when(jnp.logical_and(n >= 3, n < NCH + 3))
            def _():
                m = n - 3
                rs_msg(p, m, 1, r1, r2, r3).wait_recv()
                s3[m] = (keep[m, 1] + r2[m, 1].astype(F32)).astype(BF16)
                keep[m, 0] = keep[m, 0] + r2[m, 0].astype(F32)
                rs_msg(p, m, 2, r1, r2, r3).start()

            @pl.when(n >= 5)
            def _():
                m = n - 5
                rs_msg(p, m, 2, r1, r2, r3).wait_recv()
                finish(m, keep[m, 0] + r3[m].astype(F32))
            return 0

        lax.fori_loop(0, NCH + 5, body, 0)

        def drain(n, _):
            for j in range(3):
                rs_msg(p, n, j, r1, r2, r3).wait_send()
            return 0
        lax.fori_loop(0, NCH, drain, 0)

    def layer_norm(load, g_ref, c_ref, hg):
        stats = []
        for b in range(B):
            xf = load(b).astype(F32)
            mean = jnp.mean(xf, axis=-1, keepdims=True)
            cen = xf - mean
            var = jnp.mean(cen * cen, axis=-1, keepdims=True)
            stats.append((mean, lax.rsqrt(var + LN_EPS)))
        for u in range(NU):
            cols = slice(u * KC, (u + 1) * KC)
            for b in range(B):
                mean, rstd = stats[b]
                h = (load(b, cols).astype(F32) - mean) * rstd * g_ref[:, cols] + c_ref[:, cols]
                hg[u, me, b * S_LOC:(b + 1) * S_LOC, :] = h.astype(BF16)

    x_copy = pltpu.make_async_copy(x_hbm, xv, x_sem)
    x_copy.start()
    for i in range(NS):
        start_tile(i)
    barrier = pltpu.get_barrier_semaphore()
    for other in (sis, n1, n2):
        pl.semaphore_signal(barrier, inc=1, device_id={"tp": other}, device_id_type=MESH)
    pl.semaphore_wait(barrier, 3)
    x_copy.wait()

    layer_norm(lambda b, cols=slice(None): xv[b, :, cols], g1_ref, c1_ref, hg1)
    ag_own(0, hg1, 0)
    ag_own(0, hg1, 1)

    acc[:, 0:3 * NQ] = jnp.zeros((M, 3 * NQ), F32)

    def qkv_chunk(u):
        lhs = rows2d(hg1[u])
        for t in range(3):
            i = u * 3 + t
            w = wait_tile(i)
            acc[:, t * NQ:(t + 1) * NQ] += jnp.dot(lhs, w[...], preferred_element_type=F32)
            start_tile(i + NS)

    def qkv_body(u, _):
        ag_step(0, hg1, u, qkv_chunk)
        return 0
    lax.fori_loop(0, NU + 2, qkv_body, 0)
    ag_drain(0, hg1)

    for t in range(3):
        bias = bq_ref[t].astype(F32)
        for h in range(HEADS):
            c0 = (t * HEADS + h) * HD
            v = acc[:, c0:c0 + HD] + bias[h:h + 1, :]
            qkv[:, :, :, c0:c0 + HD] = v.astype(BF16).reshape(N_DEV, B, S_LOC, HD)

    seq = N_DEV * S_LOC
    causal = lax.broadcasted_iota(jnp.int32, (seq, seq), 0) >= lax.broadcasted_iota(jnp.int32, (seq, seq), 1)

    def attn_body(h, _):
        for b in range(B):
            def head(t):
                c0 = pl.multiple_of((t * HEADS + h) * HD, HD)
                return rows2d(qkv[:, b, :, pl.ds(c0, HD)])
            q, k, v = head(0), head(1), head(2)
            logits = lax.dot_general(q, k, (((1,), (1,)), ((), ())), preferred_element_type=F32) * HD ** -0.5
            logits = jnp.where(causal, logits, -1e30)
            e = jnp.exp(logits - jnp.max(logits, axis=-1, keepdims=True))
            w = (e / jnp.sum(e, axis=-1, keepdims=True)).astype(BF16)
            o = jnp.dot(w, v, preferred_element_type=F32).astype(BF16)
            ctx[:, b, :, pl.ds(pl.multiple_of(h * HD, HD), HD)] = o.reshape(N_DEV, S_LOC, HD)
        return 0
    lax.fori_loop(0, HEADS, attn_body, 0)

    def out_product(n, slot):
        w = wait_tile(T_QKV + n, NQ)
        part[slot] = jnp.dot(rows2d(ctx[...]), w[0:NQ, :], preferred_element_type=F32).reshape(N_DEV, ROWS, NC)
        start_tile(T_QKV + n + NS)

    def out_finish(n, total):
        cols = pl.ds(pl.multiple_of(n * NC, NC), NC)
        xs = rows2d(xv[:, :, cols]).astype(F32)
        x1[:, cols] = (xs + (total + bo_ref[:, cols])).astype(BF16)

    rs_phase(0, r1a, r2a, r3a, out_product, out_finish)

    layer_norm(lambda b, cols=slice(None): x1[b * S_LOC:(b + 1) * S_LOC, cols], g2_ref, c2_ref, hg2)
    ag_own(1, hg2, 0)
    ag_own(1, hg2, 1)

    acc[...] = jnp.zeros((M, FF), F32)

    def up_chunk(u):
        lhs = rows2d(hg2[u])
        for n in range(FF // NC):
            i = T_OUT + u * (FF // NC) + n
            w = wait_tile(i)
            acc[:, n * NC:(n + 1) * NC] += jnp.dot(lhs, w[...], preferred_element_type=F32)
            start_tile(i + NS)

    def up_body(u, _):
        ag_step(1, hg2, u, up_chunk)
        return 0
    lax.fori_loop(0, NU + 2, up_body, 0)
    ag_drain(1, hg2)

    def gelu_body(d, _):
        r = pl.ds(pl.multiple_of(d * ROWS, ROWS), ROWS)
        ub[r, :] = jax.nn.gelu(acc[r, :] + bu_ref[...], approximate=True).astype(BF16)
        return 0
    lax.fori_loop(0, N_DEV, gelu_body, 0)

    def down_product(n, slot):
        for k in range(FF // KC):
            i = T_UP + n * (FF // KC) + k
            w = wait_tile(i)
            d = jnp.dot(ub[:, k * KC:(k + 1) * KC], w[...], preferred_element_type=F32).reshape(N_DEV, ROWS, NC)
            if k == 0:
                part[slot] = d
            else:
                part[slot] += d
            start_tile(i + NS)

    def down_finish(n, total):
        cols = pl.ds(pl.multiple_of(n * NC, NC), NC)
        res = x1[:, cols].astype(F32) + (total + bd_ref[:, cols])
        out_ref[:, :, cols] = res.astype(BF16).reshape(B, S_LOC, NC)

    rs_phase(1, r1b, r2b, r3b, down_product, down_finish)


def solution(mesh):
    def device_body(hidden, ln1_gain, ln1_bias, w_qkv, b_qkv, w_out, b_out, ln2_gain, ln2_bias, w_up, b_up, w_down, b_down):
        any_spec = pl.BlockSpec(memory_space=pl.ANY)
        vmem = pl.BlockSpec(memory_space=pltpu.VMEM)

        def row(v):
            return v.astype(F32).reshape(1, -1)

        rs_buf = [pltpu.VMEM((NCH, 4, ROWS, NC), BF16), pltpu.VMEM((NCH, 2, ROWS, NC), BF16), pltpu.VMEM((NCH, ROWS, NC), BF16)]
        return pl.pallas_call(
            kernel,
            out_shape=jax.ShapeDtypeStruct((B, S_LOC, D), BF16),
            in_specs=[any_spec] * 5 + [vmem] * 8,
            out_specs=vmem,
            scratch_shapes=[
                pltpu.VMEM((B, S_LOC, D), BF16),
                pltpu.VMEM((NU, N_DEV, ROWS, KC), BF16),
                pltpu.VMEM((NU, N_DEV, ROWS, KC), BF16),
                pltpu.VMEM((M, FF), F32),
                pltpu.VMEM((N_DEV, B, S_LOC, 3 * NQ), BF16),
                pltpu.VMEM((N_DEV, B, S_LOC, NQ), BF16),
                pltpu.VMEM((M, FF), BF16),
                pltpu.VMEM((2, N_DEV, ROWS, NC), F32),
                rs_buf[0], rs_buf[0], rs_buf[0],
                rs_buf[1], rs_buf[1], rs_buf[1],
                rs_buf[2], rs_buf[2], rs_buf[2],
                pltpu.VMEM((NCH, 2, ROWS, NC), F32),
                pltpu.VMEM((ROWS, D), BF16),
                pltpu.VMEM((NS, KC, NC), BF16),
                pltpu.SemaphoreType.DMA,
                pltpu.SemaphoreType.DMA((NS,)),
                pltpu.SemaphoreType.DMA((2, NU, 7)),
                pltpu.SemaphoreType.DMA((2, NU, 7)),
                pltpu.SemaphoreType.DMA((2, NCH, 3)),
                pltpu.SemaphoreType.DMA((2, NCH, 3)),
            ],
            compiler_params=pltpu.CompilerParams(collective_id=0, has_side_effects=True, vmem_limit_bytes=67_043_328),
            name="decoder_layer",
        )(hidden, jnp.transpose(w_qkv, (1, 2, 0, 3)), w_out.reshape(HEADS * HD, D), w_up, w_down,
          row(ln1_gain), row(ln1_bias), b_qkv, row(b_out), row(ln2_gain), row(ln2_bias), row(b_up), row(b_down))

    in_layout = (P("dp", "tp", None), P(), P(), P(None, None, "tp", None), P(None, "tp", None), P("tp", None, None), P(), P(), P(), P(None, "tp"), P("tp"), P("tp", None), P())
    return jax.shard_map(device_body, mesh=mesh, in_specs=in_layout, out_specs=P("dp", "tp", None), check_vma=False)
```

time: 294 us -> 157 us (0.53)
  waiting for transfers between devices: 181 us -> 0 us
  Pallas kernels: 0 us -> 151 us
  matrix products: 67.5 us -> 0 us
  between operations: 13.6 us -> 0.01 us
  other arithmetic: 14.2 us -> 3.91 us
  starting transfers between devices: 9.69 us -> 0 us
  local copies, waits for them, and re-layouts: 7.54 us -> 1.92 us
    pallas_call x0 -> x1, Pallas kernels: none -> 151 us  [device_body(): pl.pallas_call(kernel, out_shape=jax.ShapeDtypeStruct((B, S_LOC, D), BF16...]
    all_to_all x2 -> x0, waiting for transfers between devices: 109 us -> none  [scatter_sum(): received = lax.all_to_all(split_view, 'tp', 1, 1, tiled=True)]
    all_gather x2 -> x0, waiting for transfers between devices: 71.7 us -> none  [the longest x1 37.7 us: device_body(): normed_all = lax.all_gather(normed, 'tp', axis=1, tiled=True)]
    dot_general x5 -> x0, matrix products: 67.5 us -> none  [the longest x1 22.1 us: device_body(): jnp.einsum('bsd,df->bsf', mid_all, w_up, preferred_element_type=jnp.float32)]
    reduce_sum x6 -> x0, other arithmetic: 9.65 us -> none  [the longest x2 6.35 us: scatter_sum(): return jnp.sum(received.astype(jnp.float32), axis=1)]
    all_to_all x2 -> x0, starting transfers between devices: 9.47 us -> none  [scatter_sum(): received = lax.all_to_all(split_view, 'tp', 1, 1, tiled=True)]
    reshape x2 -> x0, local copies, waits for them, and re-layouts: 7.46 us -> none  [scatter_sum(): partial.astype(jnp.bfloat16)]
    convert_element_type x7 -> x0, other arithmetic: 4.29 us -> none  [the longest x2 3.29 us: layer_norm(): (centered * lax.rsqrt(variance + LN_EPS) * gain_vec + shift_vec).astype(j...]
  transfers between devices with their start and end apart: 4 -> 0, of which waited for: 4 -> 0; matrix products, arithmetic and copies ran while one was open for 0% -> 0% of each run, Pallas kernels for 0% -> 0%
where the time goes in v1:
time: 157 us
  Pallas kernels  151 us (96%)
  other arithmetic  3.91 us (2%)
  local copies, waits for them, and re-layouts  1.92 us (1%)
    pallas_call x1, Pallas kernels, device_body(): pl.pallas_call(kernel, out_shape=jax.ShapeDtypeStruct((B, S_LOC, D), BF16...  151 us
    reshape x3, other arithmetic, row(): return v.astype(F32).reshape(1, -1)  3.91 us

profile of v1, /device:TPU:0, one launch (start us, length us, event | category | flops | bytes accessed | tf_op | source)
XLA Modules:
  0.0 156.7 jit_solution(9677506260012091223)
XLA Ops:
  0.0 1.3 reshape.43
  1.3 1.3 reshape.41
  2.6 1.3 reshape.45
  3.9 150.9 %decoder_layer.1 = bf16[3,16,6144]{2,1,0:T(8,128)(2,1)} custom-call(bf16[3,16,6144]{2,1,0:T(8,128)(2,1)} %x_hbm.1, bf16[3,6,6144,128]{3,2,1,0:T(8,128)(2,1)} %bitcast.9, bf16[768,6144]{1,0:T(8,128)(2,1)} %bitcast.10, bf16[6144,3072]{1,0:T(8,128)(2,1)} %wu_hbm.1, bf16[3072,6144]{1,0:T(8,128)(2,1)} %wd_hbm.1, f32[1,6144]{1,0:T(1,128)} %bitcast.14, ...), custom_call_target="tpu_custom_call" | custom-call | tf_op jit(solution)/shard_map/decoder_layer/pallas_call | solution.py:340
  154.8 1.9 %copy.15 = bf16[3,16,6144]{2,1,0:T(8,128)(2,1)} copy(bf16[3,16,6144]{2,1,0:T(8,128)(2,1)} %decoder_layer.1) | data formatting | bytes 1179648

commit v2 on v1

--- a/solution.py
+++ b/solution.py
@@ -36,7 +36,7 @@
 
 
 def kernel(x_hbm, wq_hbm, wo_hbm, wu_hbm, wd_hbm, g1_ref, c1_ref, bq_ref, bo_ref, g2_ref, c2_ref, bu_ref, bd_ref, out_ref,
-           xv, hg1, hg2, acc, qkv, ctx, ub, part, s1, r1a, r1b, s2, r2a, r2b, s3, r3a, r3b, keep, x1, ring,
+           xv, hg1, hg2, acc, qkv, ctx, ub, part, s1, r1a, r1b, s2, r2a, r2b, s3, r3a, r3b, keep, x1, ring, bo_row, bd_row, bu_row,
            x_sem, w_sem, ag_send, ag_recv, rs_send, rs_recv):
     me = lax.axis_index("tp")
     core = lax.rem(me, 2)
@@ -218,13 +218,17 @@
 
     x_copy = pltpu.make_async_copy(x_hbm, xv, x_sem)
     x_copy.start()
-    for i in range(NS):
-        start_tile(i)
     barrier = pltpu.get_barrier_semaphore()
     for other in (sis, n1, n2):
         pl.semaphore_signal(barrier, inc=1, device_id={"tp": other}, device_id_type=MESH)
+    for dst, src in ((bo_row, bo_ref), (bd_row, bd_ref), (bu_row, bu_ref)):
+        wide = src[...].astype(F32)
+        for r in range(src.shape[0]):
+            dst[:, r * HD:(r + 1) * HD] = wide[r:r + 1, :]
+    x_copy.wait()
+    for i in range(NS):
+        start_tile(i)
     pl.semaphore_wait(barrier, 3)
-    x_copy.wait()
 
     layer_norm(lambda b, cols=slice(None): xv[b, :, cols], g1_ref, c1_ref, hg1)
     ag_own(0, hg1, 0)
@@ -233,12 +237,12 @@
     acc[:, 0:3 * NQ] = jnp.zeros((M, 3 * NQ), F32)
 
     def qkv_chunk(u):
+        ws = [wait_tile(u * 3 + t) for t in range(3)]
         lhs = rows2d(hg1[u])
         for t in range(3):
-            i = u * 3 + t
-            w = wait_tile(i)
-            acc[:, t * NQ:(t + 1) * NQ] += jnp.dot(lhs, w[...], preferred_element_type=F32)
-            start_tile(i + NS)
+            acc[:, t * NQ:(t + 1) * NQ] += jnp.dot(lhs, ws[t][...], preferred_element_type=F32)
+        for t in range(3):
+            start_tile(u * 3 + t + NS)
 
     def qkv_body(u, _):
         ag_step(0, hg1, u, qkv_chunk)
@@ -279,7 +283,7 @@
     def out_finish(n, total):
         cols = pl.ds(pl.multiple_of(n * NC, NC), NC)
         xs = rows2d(xv[:, :, cols]).astype(F32)
-        x1[:, cols] = (xs + (total + bo_ref[:, cols])).astype(BF16)
+        x1[:, cols] = (xs + (total + bo_row[:, cols])).astype(BF16)
 
     rs_phase(0, r1a, r2a, r3a, out_product, out_finish)
 
@@ -290,12 +294,14 @@
     acc[...] = jnp.zeros((M, FF), F32)
 
     def up_chunk(u):
+        ws = [wait_tile(T_OUT + u * 4 + n) for n in range(4)]
         lhs = rows2d(hg2[u])
-        for n in range(FF // NC):
-            i = T_OUT + u * (FF // NC) + n
-            w = wait_tile(i)
-            acc[:, n * NC:(n + 1) * NC] += jnp.dot(lhs, w[...], preferred_element_type=F32)
-            start_tile(i + NS)
+        for n in range(4):
+            for h in range(3):
+                c = n * NC + h * 256
+                acc[:, c:c + 256] += jnp.dot(lhs, ws[n][:, h * 256:(h + 1) * 256], preferred_element_type=F32)
+        for n in range(4):
+            start_tile(T_OUT + u * 4 + n + NS)
 
     def up_body(u, _):
         ag_step(1, hg2, u, up_chunk)
@@ -305,24 +311,21 @@
 
     def gelu_body(d, _):
         r = pl.ds(pl.multiple_of(d * ROWS, ROWS), ROWS)
-        ub[r, :] = jax.nn.gelu(acc[r, :] + bu_ref[...], approximate=True).astype(BF16)
+        ub[r, :] = jax.nn.gelu(acc[r, :] + bu_row[...], approximate=True).astype(BF16)
         return 0
     lax.fori_loop(0, N_DEV, gelu_body, 0)
 
     def down_product(n, slot):
-        for k in range(FF // KC):
-            i = T_UP + n * (FF // KC) + k
-            w = wait_tile(i)
-            d = jnp.dot(ub[:, k * KC:(k + 1) * KC], w[...], preferred_element_type=F32).reshape(N_DEV, ROWS, NC)
-            if k == 0:
-                part[slot] = d
-            else:
-                part[slot] += d
-            start_tile(i + NS)
+        ws = [wait_tile(T_UP + n * 3 + k) for k in range(3)]
+        for h in range(3):
+            d = sum(jnp.dot(ub[:, k * KC:(k + 1) * KC], ws[k][:, h * 256:(h + 1) * 256], preferred_element_type=F32) for k in range(3))
+            part[slot, :, :, h * 256:(h + 1) * 256] = d.reshape(N_DEV, ROWS, 256)
+        for k in range(3):
+            start_tile(T_UP + n * 3 + k + NS)
 
     def down_finish(n, total):
         cols = pl.ds(pl.multiple_of(n * NC, NC), NC)
-        res = x1[:, cols].astype(F32) + (total + bd_ref[:, cols])
+        res = x1[:, cols].astype(F32) + (total + bd_row[:, cols])
         out_ref[:, :, cols] = res.astype(BF16).reshape(B, S_LOC, NC)
 
     rs_phase(1, r1b, r2b, r3b, down_product, down_finish)
@@ -334,7 +337,10 @@
         vmem = pl.BlockSpec(memory_space=pltpu.VMEM)
 
         def row(v):
-            return v.astype(F32).reshape(1, -1)
+            return v.reshape(1, -1)
+
+        def tile(v):
+            return v.reshape(-1, HD)
 
         rs_buf = [pltpu.VMEM((NCH, 4, ROWS, NC), BF16), pltpu.VMEM((NCH, 2, ROWS, NC), BF16), pltpu.VMEM((NCH, ROWS, NC), BF16)]
         return pl.pallas_call(
@@ -357,6 +363,9 @@
                 pltpu.VMEM((NCH, 2, ROWS, NC), F32),
                 pltpu.VMEM((ROWS, D), BF16),
                 pltpu.VMEM((NS, KC, NC), BF16),
+                pltpu.VMEM((1, D), F32),
+                pltpu.VMEM((1, D), F32),
+                pltpu.VMEM((1, FF), F32),
                 pltpu.SemaphoreType.DMA,
                 pltpu.SemaphoreType.DMA((NS,)),
                 pltpu.SemaphoreType.DMA((2, NU, 7)),
@@ -364,10 +373,10 @@
                 pltpu.SemaphoreType.DMA((2, NCH, 3)),
                 pltpu.SemaphoreType.DMA((2, NCH, 3)),
             ],
-            compiler_params=pltpu.CompilerParams(collective_id=0, has_side_effects=True, vmem_limit_bytes=67_043_328),
+            compiler_params=pltpu.CompilerParams(collective_id=0, has_side_effects=True, vmem_limit_bytes=66_000_000),
             name="decoder_layer",
         )(hidden, jnp.transpose(w_qkv, (1, 2, 0, 3)), w_out.reshape(HEADS * HD, D), w_up, w_down,
-          row(ln1_gain), row(ln1_bias), b_qkv, row(b_out), row(ln2_gain), row(ln2_bias), row(b_up), row(b_down))
+          row(ln1_gain), row(ln1_bias), b_qkv, tile(b_out), row(ln2_gain), row(ln2_bias), tile(b_up), tile(b_down))
 
     in_layout = (P("dp", "tp", None), P(), P(), P(None, None, "tp", None), P(None, "tp", None), P("tp", None, None), P(), P(), P(), P(None, "tp"), P("tp"), P("tp", None), P())
     return jax.shard_map(device_body, mesh=mesh, in_specs=in_layout, out_specs=P("dp", "tp", None), check_vma=False)

time: 157 us -> 132 us (0.84)
  Pallas kernels: 151 us -> 130 us
  other arithmetic: 3.91 us -> 0 us
    pallas_call x1, Pallas kernels: 151 us -> 130 us  [device_body(): pl.pallas_call(kernel, out_shape=jax.ShapeDtypeStruct((B, S_LOC, D), BF16...]
    reshape x3 -> x0, other arithmetic: 3.91 us -> none  [row(): return v.astype(F32).reshape(1, -1)]
where the time goes in v2:
time: 132 us
  Pallas kernels  130 us (98%)
  local copies, waits for them, and re-layouts  1.92 us (1%)
    pallas_call x1, Pallas kernels, device_body(): pl.pallas_call(kernel, out_shape=jax.ShapeDtypeStruct((B, S_LOC, D), BF16...  130 us

profile of v2, /device:TPU:0, one launch (start us, length us, event | category | flops | bytes accessed | tf_op | source)
XLA Modules:
  0.0 131.8 jit_solution(2804664720571406437)
XLA Ops:
  0.0 129.9 %decoder_layer.1 = bf16[3,16,6144]{2,1,0:T(8,128)(2,1)} custom-call(bf16[3,16,6144]{2,1,0:T(8,128)(2,1)} %x_hbm.1, bf16[3,6,6144,128]{3,2,1,0:T(8,128)(2,1)} %bitcast.9, bf16[768,6144]{1,0:T(8,128)(2,1)} %bitcast.10, bf16[6144,3072]{1,0:T(8,128)(2,1)} %wu_hbm.1, bf16[3072,6144]{1,0:T(8,128)(2,1)} %wd_hbm.1, f32[1,6144]{1,0:T(1,128)} %bitcast.11, ...), custom_call_target="tpu_custom_call" | custom-call | tf_op jit(solution)/shard_map/decoder_layer/pallas_call | solution.py:346
  129.9 1.9 %copy.15 = bf16[3,16,6144]{2,1,0:T(8,128)(2,1)} copy(bf16[3,16,6144]{2,1,0:T(8,128)(2,1)} %decoder_layer.1) | data formatting | bytes 1179648
